TPU v7x, 32 devices: a whole 2x2x4 slice. The times are simulated.
32 devices in a mesh: slab: 4 (over x, core), rep: 8 (over z, y).
Axes of the slice: x: 2, y: 2, z: 4, core: 2. Of those that a mesh axis runs over, the one named last changes fastest.
Arguments:
- image: float32 [144, 256, 256], P('slab', 'rep'), may hold values from 0.5 to 2
- sensitivity: float32 [144, 256, 256], P('slab', 'rep'), may hold values from 0.5 to 2
- system_blocks: bfloat16 [512, 128, 1024], P(('slab', 'rep')), may hold values from 0 to 0.00390625
- tile_slab: int32 [512, 1], P(('slab', 'rep')), may hold values from 0 to 3; in each aligned block of 16 rows (0 to 15, 16 to 31, ...) at most 6 rows name the same one
- tile_block: int32 [512], P(('slab', 'rep')), may hold values from 0 to 2303
- background: bfloat16 [512, 128], P(('slab', 'rep')), may hold values from 0.19921875 to 1
Outputs:
- updated: float32 [144, 256, 256], P('slab', 'rep')
Inputs may be any that keep to these rules, and one draw needn't show every extreme that they name: `tile_slab`: among the 16 tiles of one device at most 6 view the same slab, and in some devices some slab is viewed by exactly 6.
All inputs are finite; a program needn't handle non-finite values.
Results may differ from a plain program's by a relative error of at most 0.0003.
Values may be sent and summed in bfloat16 or wider, within the bound.
No kernel may reach another device: no remote copies, remote signals or barrier semaphores. Data moves between devices by JAX's collectives and lax.ppermute only.
A program may use at most 64 MiB of HBM per device.

v0:
```python
import jax
import jax.numpy as jnp
from jax import lax
from jax.sharding import PartitionSpec as P

CAP = 6


def local(image, sensitivity, system_blocks, tile_slab, tile_block, background):
    slab_count = lax.axis_size("slab")
    tiles_here, tile_rows, width = system_blocks.shape
    destination = tile_slab[:, 0]
    replica_total = lax.axis_size("rep")
    detector_plane_count, local_rows, column_count = image.shape
    local_blocks = image.astype(jnp.bfloat16).reshape(-1, width)
    per_plane = local_rows * replica_total * column_count // width
    per_owner = local_rows * column_count // width
    within = tile_block % per_plane
    plane_of = tile_block // per_plane
    owner_rep = within // per_owner
    local_id = plane_of * per_owner + within % per_owner
    key = destination * replica_total + owner_rep
    key_hot = (
        key[:, None] == jnp.arange(slab_count * replica_total, dtype=jnp.int32)[None, :]
    ).astype(jnp.int32)
    position_order = jnp.sum((jnp.cumsum(key_hot, axis=0) - key_hot) * key_hot, axis=1)
    id_buffer = (
        jnp.zeros((slab_count, replica_total, CAP), jnp.int32)
        .at[destination, owner_rep, position_order]
        .set(local_id)
    )
    asked = lax.all_to_all(
        lax.all_to_all(id_buffer, "slab", split_axis=0, concat_axis=0, tiled=True),
        "rep",
        split_axis=1,
        concat_axis=1,
        tiled=True,
    )
    served_requests = local_blocks[asked]
    returned = lax.all_to_all(
        lax.all_to_all(served_requests, "slab", split_axis=0, concat_axis=0, tiled=True),
        "rep",
        split_axis=1,
        concat_axis=1,
        tiled=True,
    )
    emission_cell_entries = returned[destination, owner_rep, position_order]
    forward_projection = jnp.einsum(
        "tev,tv->te", system_blocks, emission_cell_entries, preferred_element_type=jnp.float32
    )
    inverse_permutation = (1.0 / (forward_projection + background.astype(jnp.float32))).astype(
        jnp.bfloat16
    )
    own_back = jnp.einsum(
        "tev,te->tv", system_blocks, inverse_permutation, preferred_element_type=jnp.float32
    )
    back_buffer = (
        jnp.zeros((slab_count, replica_total, CAP, width), jnp.float32)
        .at[destination, owner_rep, position_order]
        .set(own_back)
    )
    received_tiles = lax.all_to_all(
        lax.all_to_all(back_buffer, "slab", split_axis=0, concat_axis=0, tiled=True),
        "rep",
        split_axis=1,
        concat_axis=1,
        tiled=True,
    )
    owned = (
        jnp.zeros(local_blocks.shape, jnp.float32)
        .at[asked.reshape(-1)]
        .add(received_tiles.reshape(-1, width))
    )
    return image * owned.reshape(image.shape) / sensitivity


def solution(mesh):
    return jax.shard_map(
        local,
        mesh=mesh,
        in_specs=(
            P("slab", "rep", None),
            P("slab", "rep", None),
            P(("slab", "rep"), None, None),
            P(("slab", "rep"), None),
            P(("slab", "rep")),
            P(("slab", "rep"), None),
        ),
        out_specs=P("slab", "rep", None),
        check_vma=False,
    )
```

profile of v0, /device:TPU:0, one launch (start us, length us, event | category | flops | bytes accessed | tf_op | source)
XLA Modules:
  0.0 104.5 jit_solution(2315465785091688998)
XLA Ops:
  0.0 0.8 fusion.8
  0.8 0.7 bitcast_add_fusion
  1.6 0.2 select_reduce_fusion
  1.7 0.7 fusion.12
  2.4 1.5 %scatter_fusion = s32[4,8,6]{1,0,2:T(4,128)S(1)} fusion(s32[4,8,6]{1,0,2:T(4,128)S(1)} %broadcast.74, s32[16]{0:T(128)S(1)} %get-tuple-element.8, s32[16]{0:T(128)S(1)} %get-tuple-element.5), kind=kCustom, calls=%fused_computation.2 | custom fusion | bytes 384 | tf_op jit(solution)/shard_map/scatter | solution.py:30
  3.9 7.9 %all_to_all.30 = s32[4,8,6]{1,2,0:T(8,128)S(1)} all-to-all(s32[4,8,6]{1,2,0:T(8,128)S(1)} %copy.23), channel_id=1, replica_groups=mesh['slab'=4,'rep'=8] {'slab'}, dimensions={0} | all-to-all | bytes 1536 | tf_op jit(solution)/shard_map/all_to_all | solution.py:33
  11.8 0.7 copy.24
  12.5 5.8 %all-to-all-start.1 = ((s32[4,8,6]{2,0,1:T(4,128)}), s32[4,8,6]{2,0,1:T(4,128)S(1)}, u32[]{:S(2)}, u32[]{:S(2)}) async-start(s32[4,8,6]{2,0,1:T(4,128)} %copy.24), calls=%async_computation.1 | async-start | bytes 32768 | tf_op jit(solution)/shard_map/all_to_all | solution.py:32
  18.5 0.4 reshape.57
  18.8 6.1 %all-to-all-done.1 = s32[4,8,6]{2,0,1:T(4,128)S(1)} async-done(((s32[4,8,6]{2,0,1:T(4,128)}), s32[4,8,6]{2,0,1:T(4,128)S(1)}, u32[]{:S(2)}, u32[]{:S(2)}) %all-to-all-start.1) | async-done | bytes 800 | tf_op jit(solution)/shard_map/all_to_all | solution.py:32
  24.9 0.1 copy.26
  25.1 0.1 copy.29
  25.3 1.0 gather_fusion
  26.3 0.1 reshape.61
  26.4 0.2 copy.30
  26.7 9.8 %all_to_all.31 = bf16[4,8,6,1024]{3,1,2,0:T(8,128)(2,1)S(1)} all-to-all(bf16[4,8,6,1024]{3,1,2,0:T(8,128)(2,1)S(1)} %copy.30), channel_id=1, replica_groups=mesh['slab'=4,'rep'=8] {'slab'}, dimensions={0} | all-to-all | bytes 786432 | tf_op jit(solution)/shard_map/all_to_all | solution.py:41
  36.5 0.3 copy.31
  36.8 14.4 %all_to_all.32 = bf16[4,8,6,1024]{3,0,2,1:T(4,128)(2,1)S(1)} all-to-all(bf16[4,8,6,1024]{3,0,2,1:T(4,128)(2,1)S(1)} %copy.31), channel_id=1, replica_groups=mesh['slab'=4,'rep'=8] {'rep'}, dimensions={1} | all-to-all | bytes 786432 | tf_op jit(solution)/shard_map/all_to_all | solution.py:40
  51.2 0.2 copy.32
  51.4 0.7 gather_fusion.1
  52.1 3.5 %fusion.2 = f32[16,1,128]{2,1,0:T(1,128)S(1)} fusion(bf16[16,128,1024]{2,1,0:T(8,128)(2,1)} %param.8, bf16[16,1024,1]{1,0,2:T(8,128)(2,1)S(1)} %bitcast.32), kind=kOutput, calls=%fused_computation.9 | convolution fusion | flops 4194304 | bytes 4235264 | tf_op jit(solution)/shard_map/tev,tv->te/dot_general | solution.py:48
  55.7 0.7 fusion.4
  56.4 1.6 %scatter_fusion.1 = f32[4,8,6,1024]{3,1,2,0:T(8,128)S(1)} fusion(f32[4,8,6,1024]{3,1,2,0:T(8,128)S(1)} %broadcast_in_dim.10, s32[16]{0:T(128)S(1)} %get-tuple-element.8, f32[16,1024]{1,0:T(8,128)S(1)} %bitcast.33), kind=kCustom, calls=%fused_computation.3 | custom fusion | bytes 196800 | tf_op jit(solution)/shard_map/scatter | solution.py:60
  58.0 14.0 %all_to_all.33 = f32[4,8,6,1024]{3,1,2,0:T(8,128)S(1)} all-to-all(f32[4,8,6,1024]{3,1,2,0:T(8,128)S(1)} %scatter_fusion.1), channel_id=1, replica_groups=mesh['slab'=4,'rep'=8] {'slab'}, dimensions={0} | all-to-all | bytes 1572864 | tf_op jit(solution)/shard_map/all_to_all | solution.py:63
  72.1 1.4 %copy.33 = f32[4,8,6,1024]{3,0,2,1:T(4,128)} copy(f32[4,8,6,1024]{3,1,2,0:T(8,128)S(1)} %all_to_all.33) | data formatting | bytes 1572864 | tf_op jit(solution)/shard_map/all_to_all | solution.py:63
  73.5 3.5 %all-to-all-start.5 = ((f32[4,8,6,1024]{3,0,2,1:T(4,128)}), f32[4,8,6,1024]{3,0,2,1:T(4,128)S(1)}, u32[]{:S(2)}, u32[]{:S(2)}) async-start(f32[4,8,6,1024]{3,0,2,1:T(4,128)} %copy.33), calls=%async_computation.5 | async-start | bytes 1572864 | tf_op jit(solution)/shard_map/all_to_all | solution.py:62
  77.2 19.9 %all-to-all-done.5 = f32[4,8,6,1024]{3,0,2,1:T(4,128)S(1)} async-done(((f32[4,8,6,1024]{3,0,2,1:T(4,128)}), f32[4,8,6,1024]{3,0,2,1:T(4,128)S(1)}, u32[]{:S(2)}, u32[]{:S(2)}) %all-to-all-start.5) | async-done | bytes 786464 | tf_op jit(solution)/shard_map/all_to_all | solution.py:62
  97.1 0.5 copy.34
  97.6 1.0 reshape.90
  98.6 3.0 %scatter_custom_fusion.2 = f32[288,1024]{1,0:T(8,128)S(1)} fusion(s32[192]{0:T(256)S(1)} %bitcast.36, f32[192,1024]{1,0:T(8,128)} %reshape.90, f32[]{:T(128)} %constant.55.clone.1), kind=kCustom, calls=%fused_computation.6 | custom fusion | flops 196608 | bytes 1180160 | tf_op jit(solution)/shard_map/scatter-add | solution.py:72
  101.6 0.3 reshape.59
  101.9 2.6 %multiply_divide_fusion = f32[36,32,256]{2,1,0:T(8,128)} fusion(f32[36,32,256]{2,1,0:T(8,128)} %param.7, f32[36,32,256]{2,1,0:T(8,128)S(1)} %copy-done.1, f32[36,32,256]{2,1,0:T(8,128)S(1)} %reshape.59), kind=kLoop, calls=%fused_computation.5 | loop fusion | flops 589824 | bytes 4718592 | tf_op jit(solution)/shard_map/div | solution.py:74
  (20 shorter events, 0.5 us)
Async XLA Ops:
  0.0 18.4 %copy-start.1 = (f32[36,32,256]{2,1,0:T(8,128)S(1)}, f32[36,32,256]{2,1,0:T(8,128)}, u32[]{:S(2)}) copy-start(f32[36,32,256]{2,1,0:T(8,128)} %param.6) | copy-start | bytes 3538948
  12.5 12.4 %all-to-all-start.1 = ((s32[4,8,6]{2,0,1:T(4,128)}), s32[4,8,6]{2,0,1:T(4,128)S(1)}, u32[]{:S(2)}, u32[]{:S(2)}) async-start(s32[4,8,6]{2,0,1:T(4,128)} %copy.24), calls=%async_computation.1 | async-start | bytes 32768 | tf_op jit(solution)/shard_map/all_to_all | solution.py:32
  52.1 3.5 %copy-start.2 = (bf16[16,128]{1,0:T(8,128)(2,1)S(1)}, bf16[16,128]{1,0:T(8,128)(2,1)}, u32[]{:S(2)}) copy-start(bf16[16,128]{1,0:T(8,128)(2,1)} %param.11) | copy-start | bytes 12292
  52.1 3.6 %copy-start = (bf16[16,128,1024]{2,1,0:T(8,128)(2,1)S(1)}, bf16[16,128,1024]{2,1,0:T(8,128)(2,1)}, u32[]{:S(2)}) copy-start(bf16[16,128,1024]{2,1,0:T(8,128)(2,1)} %param.8) | copy-start | bytes 12582916
  73.5 23.6 %all-to-all-start.5 = ((f32[4,8,6,1024]{3,0,2,1:T(4,128)}), f32[4,8,6,1024]{3,0,2,1:T(4,128)S(1)}, u32[]{:S(2)}, u32[]{:S(2)}) async-start(f32[4,8,6,1024]{3,0,2,1:T(4,128)} %copy.33), calls=%async_computation.5 | async-start | bytes 1572864 | tf_op jit(solution)/shard_map/all_to_all | solution.py:62
where the time goes:
time: 105 us
  blocking collectives  46.1 us (44%)
  waiting for transfers between devices  26.1 us (25%)
  local copies, waits for them, and re-layouts  10.5 us (10%)
  starting transfers between devices  9.38 us (9%)
  other arithmetic  8.13 us (8%)
  matrix products  4.17 us (4%)
    all_to_all x1, waiting for transfers between devices, local(): lax.all_to_all(lax.all_to_all(back_buffer, 'slab', split_axis=0, concat_a...  19.9 us
    all_to_all x1, blocking collectives, local(): lax.all_to_all(lax.all_to_all(served_requests, 'slab', split_axis=0, conc...  14.4 us
    all_to_all x1, blocking collectives, local(): lax.all_to_all(back_buffer, 'slab', split_axis=0, concat_axis=0, tiled=True)  14 us
    all_to_all x1, blocking collectives, local(): lax.all_to_all(served_requests, 'slab', split_axis=0, concat_axis=0, tile...  9.8 us
    all_to_all x1, blocking collectives, local(): lax.all_to_all(id_buffer, 'slab', split_axis=0, concat_axis=0, tiled=True)  7.9 us
    all_to_all x1, waiting for transfers between devices, local(): lax.all_to_all(lax.all_to_all(id_buffer, 'slab', split_axis=0, concat_axi...  6.12 us
    all_to_all x1, starting transfers between devices, local(): lax.all_to_all(lax.all_to_all(id_buffer, 'slab', split_axis=0, concat_axi...  5.83 us
    all_to_all x1, starting transfers between devices, local(): lax.all_to_all(lax.all_to_all(back_buffer, 'slab', split_axis=0, concat_a...  3.55 us
  transfers between devices with their start and end apart: 2, of which 2 were waited for; matrix products, arithmetic and copies ran while one was open for 1% of the time, Pallas kernels for 0%

commit v1 on v0

--- a/solution.py
+++ b/solution.py
@@ -59,12 +59,20 @@
         .at[destination, owner_rep, position_order]
         .set(own_back)
     )
-    received_tiles = lax.all_to_all(
-        lax.all_to_all(back_buffer, "slab", split_axis=0, concat_axis=0, tiled=True),
-        "rep",
-        split_axis=1,
-        concat_axis=1,
-        tiled=True,
+    received_tiles = jnp.concatenate(
+        lax.all_to_all(
+            jnp.stack(
+                jnp.split(
+                    lax.all_to_all(back_buffer, "slab", split_axis=0, concat_axis=0, tiled=True),
+                    lax.psum(1, "rep"),
+                    axis=1,
+                )
+            ),
+            "rep",
+            0,
+            0,
+        ),
+        axis=1,
     )
     owned = (
         jnp.zeros(local_blocks.shape, jnp.float32)

time: 105 us -> 109 us (1.038)
  local copies, waits for them, and re-layouts: 10.5 us -> 14.6 us
    unnamed x6 -> x13, local copies, waits for them, and re-layouts: 0.02 us -> 5.07 us
    all_to_all x2 -> x0, local copies, waits for them, and re-layouts: 1.86 us -> none  [the longest x1 1.39 us: local(): lax.all_to_all(back_buffer, 'slab', split_axis=0, concat_axis=0, tiled=True)]
    another operation x1 -> x3, local copies, waits for them, and re-layouts: 0.01 us -> 1.72 us  [the longest x1 0.99 us: local(): received_tiles.reshape(-1, width)]
where the time goes in v1:
time: 109 us
  blocking collectives  46.1 us (42%)
  waiting for transfers between devices  26.1 us (24%)
  local copies, waits for them, and re-layouts  14.6 us (13%)
  starting transfers between devices  9.38 us (9%)
  other arithmetic  8.13 us (7%)
  matrix products  4.17 us (4%)
    all_to_all x1, waiting for transfers between devices, local(): lax.all_to_all(jnp.stack(jnp.split(lax.all_to_all(back_buffer, 'slab', sp...  19.9 us
    all_to_all x1, blocking collectives, local(): lax.all_to_all(lax.all_to_all(served_requests, 'slab', split_axis=0, conc...  14.4 us
    all_to_all x1, blocking collectives, local(): lax.all_to_all(back_buffer, 'slab', split_axis=0, concat_axis=0, tiled=True)  14 us
    all_to_all x1, blocking collectives, local(): lax.all_to_all(served_requests, 'slab', split_axis=0, concat_axis=0, tile...  9.8 us
    all_to_all x1, blocking collectives, local(): lax.all_to_all(id_buffer, 'slab', split_axis=0, concat_axis=0, tiled=True)  7.9 us
    all_to_all x1, waiting for transfers between devices, local(): lax.all_to_all(lax.all_to_all(id_buffer, 'slab', split_axis=0, concat_axi...  6.12 us
    all_to_all x1, starting transfers between devices, local(): lax.all_to_all(lax.all_to_all(id_buffer, 'slab', split_axis=0, concat_axi...  5.83 us
    unnamed x13, local copies, waits for them, and re-layouts  5.07 us
  transfers between devices with their start and end apart: 2, of which 2 were waited for; matrix products, arithmetic and copies ran while one was open for 1% of the time, Pallas kernels for 0%

profile of v1, /device:TPU:0, one launch (start us, length us, event | category | flops | bytes accessed | tf_op | source)
XLA Modules:
  0.0 108.7 jit_solution(15524404668381821218)
XLA Ops:
  0.0 0.8 fusion.16
  0.8 0.7 bitcast_add_fusion
  1.7 0.7 fusion.20
  2.4 1.5 %scatter_fusion = s32[4,8,6]{1,0,2:T(4,128)S(1)} fusion(s32[4,8,6]{1,0,2:T(4,128)S(1)} %broadcast.74, s32[16]{0:T(128)S(1)} %get-tuple-element.8, s32[16]{0:T(128)S(1)} %get-tuple-element.5), kind=kCustom, calls=%fused_computation.2 | custom fusion | bytes 384 | tf_op jit(solution)/shard_map/scatter | solution.py:30
  3.9 7.9 %all_to_all.30 = s32[4,8,6]{1,2,0:T(8,128)S(1)} all-to-all(s32[4,8,6]{1,2,0:T(8,128)S(1)} %copy.22), channel_id=1, replica_groups=mesh['slab'=4,'rep'=8] {'slab'}, dimensions={0} | all-to-all | bytes 1536 | tf_op jit(solution)/shard_map/all_to_all | solution.py:33
  11.8 0.7 copy.23
  12.5 5.8 %all-to-all-start.1 = ((s32[4,8,6]{2,0,1:T(4,128)}), s32[4,8,6]{2,0,1:T(4,128)S(1)}, u32[]{:S(2)}, u32[]{:S(2)}) async-start(s32[4,8,6]{2,0,1:T(4,128)} %copy.23), calls=%async_computation.1 | async-start | bytes 32768 | tf_op jit(solution)/shard_map/all_to_all | solution.py:32
  18.5 0.4 reshape.57
  18.8 6.1 %all-to-all-done.1 = s32[4,8,6]{2,0,1:T(4,128)S(1)} async-done(((s32[4,8,6]{2,0,1:T(4,128)}), s32[4,8,6]{2,0,1:T(4,128)S(1)}, u32[]{:S(2)}, u32[]{:S(2)}) %all-to-all-start.1) | async-done | bytes 800 | tf_op jit(solution)/shard_map/all_to_all | solution.py:32
  25.3 1.0 gather_fusion
  26.7 9.8 %all_to_all.31 = bf16[4,8,6,1024]{3,1,2,0:T(8,128)(2,1)S(1)} all-to-all(bf16[4,8,6,1024]{3,1,2,0:T(8,128)(2,1)S(1)} %copy.29), channel_id=1, replica_groups=mesh['slab'=4,'rep'=8] {'slab'}, dimensions={0} | all-to-all | bytes 786432 | tf_op jit(solution)/shard_map/all_to_all | solution.py:41
  36.5 0.3 copy.30
  36.8 14.4 %all_to_all.32 = bf16[4,8,6,1024]{3,0,2,1:T(4,128)(2,1)S(1)} all-to-all(bf16[4,8,6,1024]{3,0,2,1:T(4,128)(2,1)S(1)} %copy.30), channel_id=1, replica_groups=mesh['slab'=4,'rep'=8] {'rep'}, dimensions={1} | all-to-all | bytes 786432 | tf_op jit(solution)/shard_map/all_to_all | solution.py:40
  51.4 0.7 gather_fusion.1
  52.1 3.5 %fusion.10 = f32[16,1,128]{2,1,0:T(1,128)S(1)} fusion(bf16[16,128,1024]{2,1,0:T(8,128)(2,1)} %param.8, bf16[16,1024,1]{1,0,2:T(8,128)(2,1)S(1)} %bitcast.68), kind=kOutput, calls=%fused_computation.25 | convolution fusion | flops 4194304 | bytes 4235264 | tf_op jit(solution)/shard_map/tev,tv->te/dot_general | solution.py:48
  55.7 0.7 fusion.12
  56.4 1.6 %scatter_fusion.1 = f32[4,8,6,1024]{3,1,2,0:T(8,128)S(1)} fusion(f32[4,8,6,1024]{3,1,2,0:T(8,128)S(1)} %broadcast_in_dim.10, s32[16]{0:T(128)S(1)} %get-tuple-element.8, f32[16,1024]{1,0:T(8,128)S(1)} %bitcast.69), kind=kCustom, calls=%fused_computation.3 | custom fusion | bytes 196800 | tf_op jit(solution)/shard_map/scatter | solution.py:60
  58.0 14.0 %all_to_all.33 = f32[4,8,6,1024]{3,1,2,0:T(8,128)S(1)} all-to-all(f32[4,8,6,1024]{3,1,2,0:T(8,128)S(1)} %scatter_fusion.1), channel_id=1, replica_groups=mesh['slab'=4,'rep'=8] {'slab'}, dimensions={0} | all-to-all | bytes 1572864 | tf_op jit(solution)/shard_map/all_to_all | solution.py:66
  72.1 0.7 fusion.9
  72.8 0.7 fusion.8
  73.5 0.7 fusion.7
  74.2 0.7 fusion.6
  75.0 0.7 fusion.5
  75.7 0.7 fusion.4
  76.4 0.7 fusion.3
  77.1 0.7 fusion.2
  77.9 3.5 %all-to-all-start.5 = ((f32[8,4,1,6,1024]{4,2,3,1,0:T(1,128)}), f32[8,4,1,6,1024]{4,2,3,1,0:T(1,128)S(1)}, u32[]{:S(2)}, u32[]{:S(2)}) async-start(f32[8,4,1,6,1024]{4,2,3,1,0:T(1,128)} %fusion.2), calls=%async_computation.5 | async-start | bytes 1572864 | tf_op jit(solution)/shard_map/all_to_all | solution.py:63
  81.6 19.9 %all-to-all-done.5 = f32[8,4,1,6,1024]{4,2,3,1,0:T(1,128)S(1)} async-done(((f32[8,4,1,6,1024]{4,2,3,1,0:T(1,128)}), f32[8,4,1,6,1024]{4,2,3,1,0:T(1,128)S(1)}, u32[]{:S(2)}, u32[]{:S(2)}) %all-to-all-start.5) | async-done | bytes 786464 | tf_op jit(solution)/shard_map/all_to_all | solution.py:63
  101.7 1.0 reshape.90
  102.7 3.0 %scatter_custom_fusion.2 = f32[288,1024]{1,0:T(8,128)S(1)} fusion(s32[192]{0:T(256)S(1)} %bitcast.72, f32[192,1024]{1,0:T(8,128)} %reshape.90, f32[]{:T(128)} %constant.55.clone.1), kind=kCustom, calls=%fused_computation.6 | custom fusion | flops 196608 | bytes 1180160 | tf_op jit(solution)/shard_map/scatter-add | solution.py:80
  105.7 0.3 reshape.59
  106.0 2.6 %multiply_divide_fusion = f32[36,32,256]{2,1,0:T(8,128)} fusion(f32[36,32,256]{2,1,0:T(8,128)} %param.7, f32[36,32,256]{2,1,0:T(8,128)S(1)} %copy-done.1, f32[36,32,256]{2,1,0:T(8,128)S(1)} %reshape.59), kind=kLoop, calls=%fused_computation.5 | loop fusion | flops 589824 | bytes 4718592 | tf_op jit(solution)/shard_map/div | solution.py:82
  (27 shorter events, 1.7 us)
Async XLA Ops:
  0.0 18.4 %copy-start.1 = (f32[36,32,256]{2,1,0:T(8,128)S(1)}, f32[36,32,256]{2,1,0:T(8,128)}, u32[]{:S(2)}) copy-start(f32[36,32,256]{2,1,0:T(8,128)} %param.6) | copy-start | bytes 3538948
  12.5 12.4 %all-to-all-start.1 = ((s32[4,8,6]{2,0,1:T(4,128)}), s32[4,8,6]{2,0,1:T(4,128)S(1)}, u32[]{:S(2)}, u32[]{:S(2)}) async-start(s32[4,8,6]{2,0,1:T(4,128)} %copy.23), calls=%async_computation.1 | async-start | bytes 32768 | tf_op jit(solution)/shard_map/all_to_all | solution.py:32
  52.1 3.5 %copy-start.2 = (bf16[16,128]{1,0:T(8,128)(2,1)S(1)}, bf16[16,128]{1,0:T(8,128)(2,1)}, u32[]{:S(2)}) copy-start(bf16[16,128]{1,0:T(8,128)(2,1)} %param.11) | copy-start | bytes 12292
  52.1 3.6 %copy-start = (bf16[16,128,1024]{2,1,0:T(8,128)(2,1)S(1)}, bf16[16,128,1024]{2,1,0:T(8,128)(2,1)}, u32[]{:S(2)}) copy-start(bf16[16,128,1024]{2,1,0:T(8,128)(2,1)} %param.8) | copy-start | bytes 12582916
  77.9 23.6 %all-to-all-start.5 = ((f32[8,4,1,6,1024]{4,2,3,1,0:T(1,128)}), f32[8,4,1,6,1024]{4,2,3,1,0:T(1,128)S(1)}, u32[]{:S(2)}, u32[]{:S(2)}) async-start(f32[8,4,1,6,1024]{4,2,3,1,0:T(1,128)} %fusion.2), calls=%async_computation.5 | async-start | bytes 1572864 | tf_op jit(solution)/shard_map/all_to_all | solution.py:63
